TPU v7x, 256 devices: a whole 4x4x8 slice. The times are simulated.
256 devices in a mesh: obs: 64 (over z, y_hi, x), chan: 4 (over y_lo, core).
Axes of the slice: x: 4, y: 4 (y_hi: 2, y_lo: 2; y = y_hi * 2 + y_lo), z: 8, core: 2. Of those that a mesh axis runs over, the one named last changes fastest.
Arguments:
- departures: bfloat16 [8192, 131072], P('chan', 'obs'), may hold values from -8 to 8
- predictors: bfloat16 [10, 131072], P(None, 'obs'), may hold values from -3 to 3
- inv_band: bfloat16 [63, 8192], P(None, 'chan'), may hold values from -1 to 2.5
- band_id: int32 [8192], replicated, may hold values from 0 to 340, never falling along the last dimension, each value on 1 to 32 neighbouring positions
- line_counts: int32 [1024], P('obs'), may hold values from 24 to 128
Outputs:
- gram: float32 [100, 8192], P(None, ('chan', 'obs'))
- rhs: float32 [10, 8192], P(None, ('chan', 'obs'))
Inputs may be any that keep to these rules, and one draw needn't show every extreme that they name: `band_id`: band numbers never fall along the channels; a band spans 1 to 32 channels. `line_counts`: slots of a scan line at or beyond its count are empty.
All inputs are finite; a program needn't handle non-finite values.
Results may differ from a plain program's by a relative error of at most 0.00062.
Values may be sent and summed in bfloat16 or wider, within the bound.
No kernel may reach another device: no remote copies, remote signals or barrier semaphores. Data moves between devices by JAX's collectives and lax.ppermute only.
A program may use at most 64 MiB of HBM per device.

v0:
```python
import jax
import jax.numpy as jnp
from jax import lax
from jax.sharding import PartitionSpec as P

huber_edge = 1.0


def with_halo(cells, sides, width):
    for axis, dim in sides:
        count = lax.axis_size(axis)
        ends = count - 1
        head = lax.slice_in_dim(cells, 0, width, axis=dim)
        tail = lax.slice_in_dim(cells, cells.shape[dim] - width, cells.shape[dim], axis=dim)
        cells = jnp.concatenate(
            [
                lax.ppermute(tail, axis, [(i, (i + 1) % count) for i in range(ends)]),
                cells,
                lax.ppermute(head, axis, [((i + 1) % count, i) for i in range(ends)]),
            ],
            axis=dim,
        )
    return cells


def in_blocks(value, dim, count):
    shape = value.shape
    parts = value.reshape(*shape[:dim], count, shape[dim] // count, *shape[dim + 1 :])
    return jnp.moveaxis(parts, dim, 0)


def sum_at_owner(value, axis, dim):
    parts = in_blocks(value, dim, lax.axis_size(axis))
    arrived = lax.all_to_all(parts, axis, split_axis=0, concat_axis=0, tiled=True)
    return arrived.astype(jnp.float32).sum(axis=0)


def in_one_piece(arrays, axis, dim, along):
    both = jnp.concatenate(arrays, axis=along)
    filled, at, finished = (sum_at_owner(both, axis, dim), 0, [])
    for a in arrays:
        finished.append(lax.slice_in_dim(filled, at, at + a.shape[along], axis=along))
        at += a.shape[along]
    return tuple(finished)


def on_device(departures, predictors, inv_band, band_id, line_counts):
    own, obs_dev = departures.shape
    count_pred = predictors.shape[0]
    half = inv_band.shape[0] // 2
    tile = min(256, own)
    tiles = own // tile
    extent = tile + 2 * half
    padded = with_halo(departures, (("chan", 0),), half)
    base = lax.axis_index("chan") * own
    marked = jnp.pad(band_id, (half, half), constant_values=-1)
    near_all = lax.dynamic_slice_in_dim(marked, base, own + 2 * half)
    line_slots = obs_dev // line_counts.shape[0]
    live = (
        (jnp.arange(line_slots, dtype=jnp.int32)[None, :] < line_counts[:, None])
        .reshape(obs_dev)
        .astype(jnp.float32)
    )
    band_rows = inv_band.T.reshape(tiles, tile, 2 * half + 1)
    widened = jnp.pad(band_rows, ((0, 0), (0, 0), (0, extent + 1 - (2 * half + 1))))
    skewed = widened.reshape(tiles, tile * (extent + 1))[:, : tile * extent].reshape(
        tiles, tile, extent
    )
    pieces = []
    for number in range(tiles):
        own_ids = near_all[half + number * tile : half + (number + 1) * tile]
        near_ids = near_all[number * tile : number * tile + extent]
        same = own_ids[:, None] == near_ids[None, :]
        matrix = jnp.where(same, skewed[number], jnp.zeros_like(skewed[number]))
        window = padded[number * tile : number * tile + extent]
        pieces.append(jnp.dot(matrix, window, preferred_element_type=jnp.float32))
    weighted = jnp.concatenate(pieces, axis=0)
    ratio = live[None, :] * (huber_edge / jnp.maximum(jnp.abs(weighted), huber_edge))
    qc_weight = ratio.astype(jnp.bfloat16)
    scaled = (ratio * weighted).astype(jnp.bfloat16)
    pred_wide = predictors.astype(jnp.float32)
    pairs = (
        (pred_wide[:, None, :] * pred_wide[None, :, :])
        .reshape(count_pred * count_pred, obs_dev)
        .astype(jnp.bfloat16)
    )
    factor = 1.0 / float(obs_dev * lax.axis_size("obs"))
    gram_terms = (
        jnp.einsum("ko,co->kc", pairs, qc_weight, preferred_element_type=jnp.float32) * factor
    )
    rhs_terms = (
        jnp.einsum("ko,co->kc", predictors, scaled, preferred_element_type=jnp.float32) * factor
    )
    gram_part, rhs_part = in_one_piece(
        (gram_terms.astype(jnp.bfloat16), rhs_terms.astype(jnp.bfloat16)), "obs", 1, 0
    )
    return (gram_part, rhs_part)


def solution(mesh):
    in_specs = (P("chan", "obs"), P(None, "obs"), P(None, "chan"), P(), P("obs"))
    out_specs = (P(None, ("chan", "obs")), P(None, ("chan", "obs")))
    return jax.shard_map(
        on_device, mesh=mesh, in_specs=in_specs, out_specs=out_specs, check_vma=False
    )
```

profile of v0, /device:TPU:1, one launch (start us, length us, event | category | flops | bytes accessed | tf_op | source)
XLA Modules:
  0.0 78.5 jit_solution(13482402502233052283)
XLA Ops:
  0.7 1.0 %fusion.57 = (bf16[31,2048]{1,0:T(8,128)(2,1)S(1)}, bf16[31,2048]{1,0:T(8,128)(2,1)S(1)}) fusion(bf16[2048,2048]{1,0:T(8,128)(2,1)} %param.5), kind=kLoop, calls=%fused_computation.101 | loop fusion | bytes 507904 | tf_op jit(solution)/shard_map/slice | solution.py:13
  1.7 4.6 %collective-permute-start = (bf16[31,2048]{1,0:T(8,128)(2,1)S(1)}, bf16[31,2048]{1,0:T(8,128)(2,1)S(1)}, u32[]{:S(2)}, u32[]{:S(2)}) collective-permute-start(bf16[31,2048]{1,0:T(8,128)(2,1)S(1)} %get-tuple-element.17), channel_id=1, source_target_pairs={{0,1},{1,2},{2,3},{4,5},{5,6},{6,7},{8,9},{9,10},{10,11},{12,13},{... | collective-permute-start | bytes 380936 | tf_op jit(solution)/shard_map/ppermute | solution.py:17
  6.3 1.9 %collective-permute-start.1 = (bf16[31,2048]{1,0:T(8,128)(2,1)S(1)}, bf16[31,2048]{1,0:T(8,128)(2,1)S(1)}, u32[]{:S(2)}, u32[]{:S(2)}) collective-permute-start(bf16[31,2048]{1,0:T(8,128)(2,1)S(1)} %get-tuple-element.16), channel_id=1, source_target_pairs={{1,0},{2,1},{3,2},{5,4},{6,5},{7,6},{9,8},{10,9},{11,10},{13,12},{... | collective-permute-start | bytes 380936 | tf_op jit(solution)/shard_map/ppermute | solution.py:19
  8.2 1.3 %copy.14 = bf16[2048,63]{1,0:T(8,128)(2,1)S(1)} copy(bf16[2048,63]{0,1:T(8,128)(2,1)} %bitcast.16) | data formatting | bytes 516096 | tf_op jit(solution)/shard_map/reshape | solution.py:64
  9.7 2.4 %reshape.82 = bf16[653312]{0:T(1024)(128)(2,1)S(1)} reshape(bf16[8,256,319]{2,1,0:T(8,128)(2,1)S(1)} %pad.9) | data formatting | bytes 2613248
  12.2 1.4 %reshape.71 = bf16[8,81664]{1,0:T(8,128)(2,1)S(1)} reshape(bf16[653312]{0:T(1024)(128)(2,1)S(1)} %reshape.82) | data formatting | bytes 2613248 | tf_op jit(solution)/shard_map/reshape | solution.py:66
  13.6 9.3 %slice_reduce_fusion = (bf16[81408]{0:T(1024)(128)(2,1)S(1)}, bf16[81408]{0:T(1024)(128)(2,1)S(1)}, bf16[81408]{0:T(1024)(128)(2,1)S(1)}, bf16[81408]{0:T(1024)(...) fusion(bf16[8,81664]{1,0:T(8,128)(2,1)S(1)} %reshape.71), kind=kLoop, calls=%fused_computation.39 | loop fusion | bytes 2605056 | tf_op jit(solution)/shard_map/slice | solution.py:74
  23.7 0.5 squeeze.25
  24.2 0.5 squeeze.26
  24.6 0.5 squeeze.27
  25.1 0.5 squeeze.28
  25.6 0.5 squeeze.29
  27.3 2.2 %convolution_dynamic-update-slice_fusion.7 = f32[2048,2048]{1,0:T(8,128)S(1)} fusion(bf16[2048,2048]{1,0:T(8,128)(2,1)} %param.5, bf16[31,2048]{1,0:T(8,128)(2,1)S(1)} %collective-permute-done, bf16[256,318]{1,0:T(8,128)(2,1)S(1)} %squeeze.24, s32[318]{0:T(512)S(1)} %get-tuple-element.27, s32[256]{0:T(256)S(1)} %get-tuple-element.19), kind=kOutput, calls=%fused_computation.12 | convolution fusion | flops 336215040 | bytes 10777848 | tf_op jit(solution)/shard_map/dot_general | solution.py:76
  29.5 2.2 %convolution_dynamic-update-slice_fusion.6 = f32[2048,2048]{1,0:T(8,128)S(1)} fusion(f32[2048,2048]{1,0:T(8,128)S(1)} %convolution_dynamic-update-slice_fusion.7, bf16[2048,2048]{1,0:T(8,128)(2,1)} %param.5, bf16[256,318]{1,0:T(8,128)(2,1)S(1)} %squeeze.25, s32[318]{0:T(512)S(1)} %get-tuple-element.28, s32[256]{0:T(256)S(1)} %get-tuple-element.20), kind=kOutput, calls=%fused_computation.11 | convolution fusion | flops 333609984 | bytes 3607552 | tf_op jit(solution)/shard_map/dot_general | solution.py:76
  31.8 2.1 %convolution_dynamic-update-slice_fusion.5 = f32[2048,2048]{1,0:T(8,128)S(1)} fusion(f32[2048,2048]{1,0:T(8,128)S(1)} %convolution_dynamic-update-slice_fusion.6, bf16[2048,2048]{1,0:T(8,128)(2,1)} %param.5, bf16[256,318]{1,0:T(8,128)(2,1)S(1)} %squeeze.26, s32[318]{0:T(512)S(1)} %get-tuple-element.29, s32[256]{0:T(256)S(1)} %get-tuple-element.21), kind=kOutput, calls=%fused_computation.10 | convolution fusion | flops 333609984 | bytes 3607552 | tf_op jit(solution)/shard_map/dot_general | solution.py:76
  33.9 2.1 %convolution_dynamic-update-slice_fusion.4 = f32[2048,2048]{1,0:T(8,128)S(1)} fusion(f32[2048,2048]{1,0:T(8,128)S(1)} %convolution_dynamic-update-slice_fusion.5, bf16[2048,2048]{1,0:T(8,128)(2,1)} %param.5, bf16[256,318]{1,0:T(8,128)(2,1)S(1)} %squeeze.27, s32[318]{0:T(512)S(1)} %get-tuple-element.30, s32[256]{0:T(256)S(1)} %get-tuple-element.22), kind=kOutput, calls=%fused_computation.9 | convolution fusion | flops 333609984 | bytes 3607552 | tf_op jit(solution)/shard_map/dot_general | solution.py:76
  36.0 0.8 convolution_dynamic-update-slice_fusion.3
  36.8 0.8 convolution_dynamic-update-slice_fusion.2
  37.5 0.8 convolution_dynamic-update-slice_fusion.1
  38.3 0.8 convolution_dynamic-update-slice_fusion
  39.1 3.2 %fusion.12 = bf16[10,2048]{1,0:T(8,128)(2,1)S(1)} fusion(bf16[10,2048]{1,0:T(8,128)(2,1)S(1)} %copy-done.1, f32[2048,2048]{1,0:T(8,128)S(1)} %convolution_dynamic-update-slice_fusion, f32[2048]{0:T(1024)S(1)} %convert_bitcast_fusion), kind=kOutput, calls=%fused_computation.17 | convolution fusion | flops 109092864 | bytes 16867328 | tf_op jit(solution)/shard_map/ko,co->kc/dot_general | solution.py:92
  42.3 3.3 %fusion.7 = bf16[100,2048]{1,0:T(8,128)(2,1)S(1)} fusion(bf16[100,2048]{1,0:T(8,128)(2,1)S(1)} %convert_element_type.41, f32[2048,2048]{1,0:T(8,128)S(1)} %convolution_dynamic-update-slice_fusion, f32[2048]{0:T(1024)S(1)} %convert_bitcast_fusion), kind=kOutput, calls=%fused_computation.14 | convolution fusion | flops 860241920 | bytes 17604608 | tf_op jit(solution)/shard_map/ko,co->kc/dot_general | solution.py:89
  45.9 31.7 %all_to_all.5 = bf16[64,110,32]{1,2,0:T(8,128)(2,1)S(1)} all-to-all(bf16[64,110,32]{1,2,0:T(8,128)(2,1)S(1)} %bitcast.15), channel_id=1, replica_groups=mesh['obs'=64,'chan'=4] {'obs'}, dimensions={0} | all-to-all | bytes 901120 | tf_op jit(solution)/shard_map/all_to_all | solution.py:34
  77.8 0.7 copy.13
  (29 shorter events, 2.8 us)
Async XLA Ops:
  0.6 22.2 %copy-start.3 = (s32[16]{0:T(128)S(1)}, s32[16]{0:T(128)}, u32[]{:S(2)}) copy-start(s32[16]{0:T(128)} %param.9) | copy-start | bytes 196
  0.6 22.3 %copy-start.1 = (bf16[10,2048]{1,0:T(8,128)(2,1)S(1)}, bf16[10,2048]{1,0:T(8,128)(2,1)}, u32[]{:S(2)}) copy-start(bf16[10,2048]{1,0:T(8,128)(2,1)} %param.6) | copy-start | bytes 122884
  0.7 22.4 %copy-start = (s32[8192]{0:T(1024)S(1)}, s32[8192]{0:T(1024)}, u32[]{:S(2)}) copy-start(s32[8192]{0:T(1024)} %param.8) | copy-start | bytes 98308
  1.7 25.6 %collective-permute-start = (bf16[31,2048]{1,0:T(8,128)(2,1)S(1)}, bf16[31,2048]{1,0:T(8,128)(2,1)S(1)}, u32[]{:S(2)}, u32[]{:S(2)}) collective-permute-start(bf16[31,2048]{1,0:T(8,128)(2,1)S(1)} %get-tuple-element.17), channel_id=1, source_target_pairs={{0,1},{1,2},{2,3},{4,5},{5,6},{6,7},{8,9},{9,10},{10,11},{12,13},{... | collective-permute-start | bytes 380936 | tf_op jit(solution)/shard_map/ppermute | solution.py:17
  6.3 32.0 %collective-permute-start.1 = (bf16[31,2048]{1,0:T(8,128)(2,1)S(1)}, bf16[31,2048]{1,0:T(8,128)(2,1)S(1)}, u32[]{:S(2)}, u32[]{:S(2)}) collective-permute-start(bf16[31,2048]{1,0:T(8,128)(2,1)S(1)} %get-tuple-element.16), channel_id=1, source_target_pairs={{1,0},{2,1},{3,2},{5,4},{6,5},{7,6},{9,8},{10,9},{11,10},{13,12},{... | collective-permute-start | bytes 380936 | tf_op jit(solution)/shard_map/ppermute | solution.py:19
  27.3 8.7 %slice-start = ((s8[8388608]{0:T(1024)(128)(4,1)}), s8[4194304]{0:T(1024)(128)(4,1)S(1)}, s32[]{:S(2)}) async-start(s8[8388608]{0:T(1024)(128)(4,1)} %bitcast.12), calls=%async_computation.1 | async-start | bytes 8388608
  29.5 6.5 %slice-start.1 = ((s8[8388608]{0:T(1024)(128)(4,1)}), s8[4194304]{0:T(1024)(128)(4,1)S(1)}, s32[]{:S(2)}) async-start(s8[8388608]{0:T(1024)(128)(4,1)} %bitcast.12), calls=%async_computation.2 | async-start | bytes 8388608
  77.7 0.8 copy-start.2
where the time goes:
time: 78.8 us; the launch traced here: 78.5 us
  blocking collectives  31.7 us (40%)
  local copies, waits for them, and re-layouts  20.9 us (27%)
  matrix products  18.2 us (23%)
  starting transfers between devices  6.5 us (8%)
  between operations  0.92 us (1%)
    all_to_all x1, blocking collectives, sum_at_owner(): lax.all_to_all(parts, axis, split_axis=0, concat_axis=0, tiled=True)  31.7 us
    dot_general x8, matrix products, on_device(): pieces.append(jnp.dot(matrix, window, preferred_element_type=jnp.float32))  11.7 us
    slice x1, local copies, waits for them, and re-layouts, on_device(): matrix = jnp.where(same, skewed[number], jnp.zeros_like(skewed[number]))  9.3 us
    ppermute x1, starting transfers between devices, with_halo(): lax.ppermute(tail, axis, [(i, (i + 1) % count) for i in range(ends)])  4.58 us
    squeeze x8, local copies, waits for them, and re-layouts, on_device(): matrix = jnp.where(same, skewed[number], jnp.zeros_like(skewed[number]))  3.75 us
    dot_general x1, matrix products, on_device(): jnp.einsum('ko,co->kc', pairs, qc_weight, preferred_element_type=jnp.floa...  3.25 us
    dot_general x1, matrix products, on_device(): jnp.einsum('ko,co->kc', predictors, scaled, preferred_element_type=jnp.fl...  3.25 us
    unnamed x14, local copies, waits for them, and re-layouts  3.15 us
  transfers between devices with their start and end apart: 2, of which 0 were waited for; matrix products, arithmetic and copies ran while one was open for 38% of the time, Pallas kernels for 0%

commit v1 on v0

v1 whole, which is shorter than its diff:
```python
import functools
import jax
import jax.numpy as jnp
from jax import lax
from jax.experimental import pallas as pl
from jax.experimental.pallas import tpu as pltpu
from jax.sharding import PartitionSpec as P

TILE = 128
HALO = 32
WIN = TILE + 2 * HALO
STEP = 256
OBS = 512
GROUP = 32
ROWS = 24

f32, bf16 = jnp.float32, jnp.bfloat16


def prepare_moments(pred, counts, w1_ref, w2_ref):
    count_pred, obs = pred.shape
    lines = counts.shape[0]
    slots = obs // lines
    pairs_n = count_pred * (count_pred + 1) // 2
    lane = lax.broadcasted_iota(jnp.int32, (1, slots), 1)
    column = lax.broadcasted_iota(jnp.int32, (slots, 128), 1)
    for line in range(lines):
        at = slice(line * slots, (line + 1) * slots)
        p = jnp.where(lane < counts[line], pred[:, at].astype(f32), 0.0)
        rows = [p[j : j + 1] * p[j:] for j in range(count_pred)] + [p]
        used = pairs_n + count_pred
        rows.append(jnp.zeros((128 - used, slots), f32))
        moments = jnp.concatenate(rows, axis=0).T
        w1_ref[at] = jnp.where(column < pairs_n, moments, 0.0).astype(bf16)
        w2_ref[at] = jnp.where(column >= pairs_n, moments, 0.0).astype(bf16)


def prepare_band(t, chan, inv_ref, ids_ref, band_ref):
    tiles = inv_ref.shape[1] // TILE
    total = ids_ref.shape[0]
    offsets = inv_ref.shape[0]
    at = chan * tiles + t
    own = ids_ref[pl.ds(at, 1)].astype(f32)
    before = ids_ref[pl.ds(jnp.maximum(at - 1, 0), 1)].astype(f32)
    after = ids_ref[pl.ds(jnp.minimum(at + 1, total - 1), 1)].astype(f32)
    before = jnp.where(at > 0, before, -1.0)
    after = jnp.where(at < total - 1, after, -1.0)
    near = jnp.concatenate(
        [before[:, TILE - HALO :], own, after[:, :HALO], jnp.full((1, 256 - WIN), -1.0, f32)],
        axis=1,
    )
    values = inv_ref[:, t * TILE : (t + 1) * TILE].astype(f32)
    stacked = jnp.concatenate([values, own, jnp.zeros((128 - offsets - 1, TILE), f32)], axis=0).T
    own_id = stacked[:, offsets : offsets + 1]
    column = lax.broadcasted_iota(jnp.int32, (TILE, 128), 1)
    wide = jnp.concatenate(
        [jnp.where(column < offsets, stacked, 0.0), jnp.zeros((TILE, 128), f32)], axis=1
    )
    skewed = pltpu.roll(wide, 1, 1, stride=1, stride_axis=0)
    band_ref[...] = jnp.where(own_id == near, skewed, 0.0).astype(bf16)


def weigh(window, matrix, qc_ref, scaled_ref, rows):
    for o in range(0, window.shape[1], OBS):
        at = slice(o, o + OBS)
        w = jnp.dot(matrix[:, :WIN], window[:, at], preferred_element_type=f32)
        ratio = 1.0 / jnp.maximum(jnp.abs(w), 1.0)
        qc_ref[rows, at] = ratio.astype(bf16)
        scaled_ref[rows, at] = jnp.clip(w, -1.0, 1.0).astype(bf16)


def reduce(first, qc_ref, scaled_ref, w1, w2, out_ref):
    lane = lax.broadcasted_iota(jnp.int32, (GROUP // 2, 128), 1)
    lane8 = lax.broadcasted_iota(jnp.int32, (8, 128), 1)
    total = jnp.dot(qc_ref[...], w1[...], preferred_element_type=f32)
    total += jnp.dot(scaled_ref[...], w2[...], preferred_element_type=f32)
    for g in range(STEP // GROUP):
        block = total[g * GROUP : (g + 1) * GROUP]
        low, high = block[: GROUP // 2], block[GROUP // 2 :]
        main = jnp.where(lane < 64, low, pltpu.roll(high, 64, 1))
        last = jnp.zeros((8, 128), f32)
        for v in range(GROUP // 8):
            moved = pltpu.roll(block[v * 8 : v * 8 + 8], 64 + v, 1)
            last = jnp.where(lane8 == v, moved, last)
        out_ref[first[g]] = jnp.concatenate([main, last], axis=0).astype(bf16)


def groups_of(*tiles):
    return [t * (TILE // GROUP) + g for t in tiles for g in range(TILE // GROUP)]


def inner_kernel(
    chan_ref, counts_hbm, pred_hbm, inv_hbm, ids_hbm, dep_hbm,
    out_ref, edge, edge_band, w1, w2,
    dep_all, band, qc, scaled, counts, pred, inv, ids, sems,
):
    own, obs = dep_hbm.shape
    tiles = own // TILE
    steps = tiles // 2 - 1
    chunks = own // STEP

    def copy(number, source, target):
        return pltpu.make_async_copy(source, target, sems.at[number])

    small = [
        copy(0, counts_hbm, counts),
        copy(1, pred_hbm, pred),
        copy(2, inv_hbm, inv),
        copy(3, ids_hbm, ids),
    ]
    rows = [pl.ds(s * STEP, STEP) for s in range(chunks)]
    large = [copy(4 + s, dep_hbm.at[rows[s]], dep_all.at[rows[s]]) for s in range(chunks)]
    kept = WIN - HALO
    ends = [
        copy(4 + chunks, dep_hbm.at[pl.ds(0, kept)], edge.at[0, pl.ds(HALO, kept)]),
        copy(5 + chunks, dep_hbm.at[pl.ds(own - kept, kept)], edge.at[1, pl.ds(0, kept)]),
    ]
    for c in small + large + ends:
        c.start()
    for c in small:
        c.wait()
    chan = chan_ref[0]
    prepare_moments(pred, counts, w1, w2)
    for t in range(tiles):
        if t == 0:
            prepare_band(t, chan, inv, ids, edge_band.at[0])
        elif t == tiles - 1:
            prepare_band(t, chan, inv, ids, edge_band.at[1])
        else:
            prepare_band(t, chan, inv, ids, band.at[t])
    arrived = 0
    for s in range(steps):
        needed = min(chunks, ((2 * s + 3) * TILE + HALO - 1) // STEP + 1)
        for c in large[arrived:needed]:
            c.wait()
        arrived = needed
        for half in range(2):
            t = 2 * s + 1 + half
            window = dep_all.at[pl.ds(t * TILE - HALO, WIN)]
            weigh(window, band.at[t], qc.at[s % 2], scaled.at[s % 2], pl.ds(half * TILE, TILE))
        if s > 0:
            p = s - 1
            reduce(groups_of(2 * p + 1, 2 * p + 2), qc.at[p % 2], scaled.at[p % 2], w1, w2, out_ref)
    p = steps - 1
    reduce(groups_of(2 * p + 1, 2 * p + 2), qc.at[p % 2], scaled.at[p % 2], w1, w2, out_ref)
    for c in large[arrived:] + ends:
        c.wait()


def edge_kernel(
    top_ref, bottom_ref, edge_band, w1, w2, parts_ref, edge_ref, out_ref, edge, qc, scaled
):
    tiles = parts_ref.shape[0] * GROUP // TILE
    edge[0, :HALO] = top_ref[...]
    edge[1, WIN - HALO :] = bottom_ref[...]
    for half in range(2):
        weigh(edge.at[half], edge_band.at[half], qc, scaled, pl.ds(half * TILE, TILE))
    reduce(groups_of(0, tiles - 1), qc, scaled, w1, w2, out_ref)


def border_kernel(dep_hbm, head_ref, tail_ref, sems):
    own = dep_hbm.shape[0]
    head = pltpu.make_async_copy(dep_hbm.at[pl.ds(0, HALO)], head_ref, sems.at[0])
    tail = pltpu.make_async_copy(dep_hbm.at[pl.ds(own - HALO, HALO)], tail_ref, sems.at[1])
    head.start()
    tail.start()
    head.wait()
    tail.wait()


def borders(departures):
    vmem = pl.BlockSpec(memory_space=pltpu.VMEM)
    rows = jax.ShapeDtypeStruct((HALO, departures.shape[1]), bf16)
    return pl.pallas_call(
        border_kernel,
        out_shape=(rows, rows),
        in_specs=[pl.BlockSpec(memory_space=pltpu.HBM)],
        out_specs=(vmem, vmem),
        scratch_shapes=[pltpu.SemaphoreType.DMA((2,))],
        compiler_params=pltpu.CompilerParams(vmem_limit_bytes=50 * 1024 * 1024),
        cost_estimate=pl.CostEstimate(flops=20_000_000_000, bytes_accessed=500_000, transcendentals=0),
        name="borders",
    )(departures)


def partial_sums(chan, counts, top, bottom, pred, inv_band, ids, departures):
    own, obs = departures.shape
    tiles = own // TILE
    vmem = pl.BlockSpec(memory_space=pltpu.VMEM)
    smem = pl.BlockSpec(memory_space=pltpu.SMEM)
    hbm = pl.BlockSpec(memory_space=pltpu.HBM)
    shape = jax.ShapeDtypeStruct
    parts_shape = shape((own // GROUP, ROWS, 128), bf16)
    edge_shape = shape((2, WIN, obs), bf16)
    parts, edge, edge_band, w1, w2 = pl.pallas_call(
        inner_kernel,
        out_shape=(
            parts_shape,
            edge_shape,
            shape((2, TILE, 256), bf16),
            shape((obs, 128), bf16),
            shape((obs, 128), bf16),
        ),
        in_specs=[smem, hbm, hbm, hbm, hbm, hbm],
        out_specs=(vmem,) * 5,
        scratch_shapes=[
            pltpu.VMEM((own, obs), bf16),
            pltpu.VMEM((tiles, TILE, 256), bf16),
            pltpu.VMEM((2, STEP, obs), bf16),
            pltpu.VMEM((2, STEP, obs), bf16),
            pltpu.SMEM(counts.shape, jnp.int32),
            pltpu.VMEM(pred.shape, bf16),
            pltpu.VMEM(inv_band.shape, bf16),
            pltpu.VMEM(ids.shape, jnp.int32),
            pltpu.SemaphoreType.DMA((6 + own // STEP,)),
        ],
        compiler_params=pltpu.CompilerParams(vmem_limit_bytes=50 * 1024 * 1024),
        cost_estimate=pl.CostEstimate(flops=12_000_000_000, bytes_accessed=9_000_000, transcendentals=0),
        name="inner",
    )(chan, counts, pred, inv_band, ids, departures)
    parts, _ = pl.pallas_call(
        edge_kernel,
        out_shape=(parts_shape, edge_shape),
        in_specs=[vmem] * 7,
        out_specs=(vmem, vmem),
        input_output_aliases={5: 0, 6: 1},
        scratch_shapes=[pltpu.VMEM((STEP, obs), bf16), pltpu.VMEM((STEP, obs), bf16)],
        compiler_params=pltpu.CompilerParams(vmem_limit_bytes=16 * 1024 * 1024),
        name="edge",
    )(top, bottom, edge_band, w1, w2, parts, edge)
    return parts


def finish_kernel(factor, place_ref, parts_ref, gram_ref, rhs_ref):
    count_pred = rhs_ref.shape[0]
    pairs_n = count_pred * (count_pred + 1) // 2
    half = GROUP // 2
    total = parts_ref[...].astype(f32).sum(axis=0) * factor
    main, last = total[:half], total[half:]
    lane = lax.broadcasted_iota(jnp.int32, (GROUP, 128), 1)
    joined = jnp.concatenate([main, pltpu.roll(main, 64, 1)], axis=0)
    ends = jnp.concatenate([pltpu.roll(last, 64 - v, 1) for v in range(GROUP // 8)], axis=0)
    joined = jnp.where(lane < 64, joined, ends)
    place = jnp.broadcast_to(place_ref[...], (GROUP, 128))
    gram = jnp.take_along_axis(joined, place, axis=1)
    gram_ref[...] = gram[:, : count_pred * count_pred]
    turned = jnp.concatenate([joined, jnp.zeros((128 - GROUP, 128), f32)], axis=0).T
    rhs_ref[...] = turned[pairs_n : pairs_n + count_pred, :GROUP]


def finish(parts, count_pred, factor):
    index = []
    for j in range(count_pred):
        for k in range(count_pred):
            a, b = min(j, k), max(j, k)
            index.append(a * count_pred - a * (a - 1) // 2 + b - a)
    index += [0] * (128 - len(index))
    vmem = pl.BlockSpec(memory_space=pltpu.VMEM)
    gram, rhs = pl.pallas_call(
        functools.partial(finish_kernel, factor),
        out_shape=(
            jax.ShapeDtypeStruct((GROUP, count_pred * count_pred), f32),
            jax.ShapeDtypeStruct((count_pred, GROUP), f32),
        ),
        in_specs=[vmem, vmem],
        out_specs=(vmem, vmem),
        compiler_params=pltpu.CompilerParams(vmem_limit_bytes=4 * 1024 * 1024),
        name="finish",
    )(jnp.array([index], jnp.int32), parts)
    return gram.T, rhs


def on_device(departures, predictors, inv_band, band_id, line_counts):
    own, obs = departures.shape
    count = lax.axis_size("chan")
    up = [(i, i + 1) for i in range(count - 1)]
    down = [(i + 1, i) for i in range(count - 1)]
    head, tail = borders(departures)
    top = lax.ppermute(tail, "chan", up)
    bottom = lax.ppermute(head, "chan", down)
    chan = lax.axis_index("chan").astype(jnp.int32).reshape(1)
    ids = band_id.reshape(-1, TILE)
    parts = partial_sums(chan, line_counts, top, bottom, predictors, inv_band, ids, departures)
    arrived = lax.all_to_all(parts, "obs", split_axis=0, concat_axis=0, tiled=True)
    return finish(arrived, predictors.shape[0], 1.0 / float(obs * lax.axis_size("obs")))


def solution(mesh):
    in_specs = (P("chan", "obs"), P(None, "obs"), P(None, "chan"), P(), P("obs"))
    out_specs = (P(None, ("chan", "obs")), P(None, ("chan", "obs")))
    return jax.shard_map(
        on_device, mesh=mesh, in_specs=in_specs, out_specs=out_specs, check_vma=False
    )
```

time: 78.8 us -> 50 us (0.63)
  local copies, waits for them, and re-layouts: 20.9 us -> 0.02 us
  matrix products: 18.2 us -> 0 us
  Pallas kernels: 0 us -> 13.1 us
  blocking collectives: 31.7 us -> 29.3 us
    dot_general x10 -> x0, matrix products: 18.2 us -> none  [the longest x8 11.7 us: on_device(): pieces.append(jnp.dot(matrix, window, preferred_element_type=jnp.float32))]
    pallas_call x0 -> x4, Pallas kernels: none -> 13.1 us  [the longest x1 10.1 us: partial_sums(): pl.pallas_call(inner_kernel, out_shape=(parts_shape, edge_shape, shape((2...]
    slice x5 -> x0, local copies, waits for them, and re-layouts: 10.7 us -> none  [the longest x1 9.3 us: on_device(): matrix = jnp.where(same, skewed[number], jnp.zeros_like(skewed[number]))]
    squeeze x8 -> x0, local copies, waits for them, and re-layouts: 3.75 us -> none  [on_device(): matrix = jnp.where(same, skewed[number], jnp.zeros_like(skewed[number]))]
    unnamed x14 -> x10, local copies, waits for them, and re-layouts: 3.15 us -> 0.02 us
    reshape x2 -> x0, local copies, waits for them, and re-layouts: 2.63 us -> none  [the longest x1 1.38 us: on_device(): widened.reshape(tiles, tile * (extent + 1))[:, :tile * extent]]
    all_to_all x1, blocking collectives: 31.7 us -> 29.3 us  [on_device(): lax.all_to_all(parts, 'obs', split_axis=0, concat_axis=0, tiled=True)]
  transfers between devices with their start and end apart: 2 -> 2, of which waited for: 0 -> 0; matrix products, arithmetic and copies ran while one was open for 38% -> 0% of each run, Pallas kernels for 0% -> 20%
where the time goes in v1:
time: 50 us; the launch traced here: 49.8 us
  blocking collectives  29.3 us (59%)
  Pallas kernels  13.1 us (26%)
  starting transfers between devices  6.5 us (13%)
  between operations  0.76 us (2%)
    all_to_all x1, blocking collectives, on_device(): lax.all_to_all(parts, 'obs', split_axis=0, concat_axis=0, tiled=True)  29.3 us
    pallas_call x1, Pallas kernels, partial_sums(): pl.pallas_call(inner_kernel, out_shape=(parts_shape, edge_shape, shape((2...  10.1 us
    ppermute x1, starting transfers between devices, on_device(): top = lax.ppermute(tail, 'chan', up)  4.58 us
    ppermute x1, starting transfers between devices, on_device(): bottom = lax.ppermute(head, 'chan', down)  1.92 us
    pallas_call x1, Pallas kernels, partial_sums(): pl.pallas_call(edge_kernel, out_shape=(parts_shape, edge_shape), in_specs...  1.19 us
    pallas_call x1, Pallas kernels, borders(): pl.pallas_call(border_kernel, out_shape=(rows, rows), in_specs=[pl.BlockS...  1.03 us
  transfers between devices with their start and end apart: 2, of which 0 were waited for; matrix products, arithmetic and copies ran while one was open for 0% of the time, Pallas kernels for 20%

profile of v1, /device:TPU:1, one launch (start us, length us, event | category | flops | bytes accessed | tf_op | source)
XLA Modules:
  0.0 49.8 jit_solution(3214679060118006722)
XLA Ops:
  0.6 0.0 copy-start.4
  0.6 0.0 copy-start.3
  0.7 0.0 copy-start.1
  0.7 0.0 copy-start.2
  0.7 1.0 %borders.1 = (bf16[32,2048]{1,0:T(8,128)(2,1)S(1)}, bf16[32,2048]{1,0:T(8,128)(2,1)S(1)}) custom-call(bf16[2048,2048]{1,0:T(8,128)(2,1)} %dep_hbm.3), custom_call_target="tpu_custom_call" | custom-call | flops 20000000000 | bytes 500000 | tf_op jit(solution)/shard_map/borders/pallas_call | solution.py:174
  1.7 4.6 %collective-permute-start = (bf16[32,2048]{1,0:T(8,128)(2,1)S(1)}, bf16[32,2048]{1,0:T(8,128)(2,1)S(1)}, u32[]{:S(2)}, u32[]{:S(2)}) collective-permute-start(bf16[32,2048]{1,0:T(8,128)(2,1)S(1)} %get-tuple-element.12), channel_id=1, source_target_pairs={{0,1},{1,2},{2,3},{4,5},{5,6},{6,7},{8,9},{9,10},{10,11},{12,13},{... | collective-permute-start | bytes 393224 | tf_op jit(solution)/shard_map/ppermute | solution.py:279
  6.3 1.9 %collective-permute-start.1 = (bf16[32,2048]{1,0:T(8,128)(2,1)S(1)}, bf16[32,2048]{1,0:T(8,128)(2,1)S(1)}, u32[]{:S(2)}, u32[]{:S(2)}) collective-permute-start(bf16[32,2048]{1,0:T(8,128)(2,1)S(1)} %get-tuple-element.13), channel_id=1, source_target_pairs={{1,0},{2,1},{3,2},{5,4},{6,5},{7,6},{9,8},{10,9},{11,10},{13,12},{... | collective-permute-start | bytes 393224 | tf_op jit(solution)/shard_map/ppermute | solution.py:280
  8.2 0.0 copy-done.4
  8.2 0.0 copy-done.3
  8.3 0.0 copy-done.1
  8.3 0.0 copy-done.2
  8.3 10.1 %inner.1 = (bf16[64,24,128]{2,1,0:T(8,128)(2,1)S(1)}, bf16[2,192,2048]{2,1,0:T(8,128)(2,1)S(1)}, bf16[2,128,256]{2,1,0:T(8,128)(2,1)S(1)}, bf16[2048,128]{1,0:T(8,128)(2,1)S(1)}, bf16[2048,128]{1,0:T(8,128)(2,1)S(1)}) custom-call(s32[1]{0:T(128)} %bitcast.chan_ref, s32[16]{0:T(128)S(1)} %copy-done.4, bf16[10,2048]{1,0:T(8,128)(2,1)S(1)} %copy-done.2, ...), custom_call_target="tpu_custom_call" | custom-call | flops 12000000000 | bytes 9000000 | tf_op jit(solution)/shard_map/inner/pallas_call | solution.py:195
  18.3 0.0 collective-permute-done.top_ref
  18.3 0.0 collective-permute-done.1.bottom_ref
  18.4 0.0 copy-start
  18.4 1.2 %edge.1 = (bf16[64,24,128]{2,1,0:T(8,128)(2,1)S(1)}, bf16[2,192,2048]{2,1,0:T(8,128)(2,1)S(1)}) custom-call(bf16[32,2048]{1,0:T(8,128)(2,1)S(1)} %collective-permute-done.top_ref, bf16[32,2048]{1,0:T(8,128)(2,1)S(1)} %collective-permute-done.1.bottom_ref, ...), custom_call_target="tpu_custom_call", output_to_operand_aliasing={{0}: (5, {}), {1}: (6, {})} | custom-call | tf_op jit(solution)/shard_map/edge/pallas_call | solution.py:221
  19.6 29.3 %all_to_all.5.parts_ref = bf16[64,24,128]{2,1,0:T(8,128)(2,1)S(1)} all-to-all(bf16[64,24,128]{2,1,0:T(8,128)(2,1)S(1)} %get-tuple-element.19), channel_id=1, replica_groups=mesh['obs'=64,'chan'=4] {'obs'}, dimensions={0} | all-to-all | bytes 786432 | tf_op jit(solution)/shard_map/all_to_all | solution.py:284
  48.9 0.0 copy-done
  48.9 0.9 %finish.1 = (f32[32,100]{1,0:T(8,128)}, f32[10,32]{1,0:T(8,128)}) custom-call(s32[1,128]{1,0:T(1,128)S(1)} %copy-done, bf16[64,24,128]{2,1,0:T(8,128)(2,1)S(1)} %all_to_all.5.parts_ref), custom_call_target="tpu_custom_call" | custom-call | tf_op jit(solution)/shard_map/finish/pallas_call | solution.py:259
Async XLA Ops:
  0.6 7.6 %copy-start.4 = (s32[16]{0:T(128)S(1)}, s32[16]{0:T(128)}, u32[]{:S(2)}) copy-start(s32[16]{0:T(128)} %counts_hbm.1) | copy-start | bytes 196
  0.6 7.6 %copy-start.3 = (s32[8192]{0:T(1024)S(1)}, s32[8192]{0:T(1024)}, u32[]{:S(2)}) copy-start(s32[8192]{0:T(1024)} %param.9) | copy-start | bytes 98308
  0.7 7.6 %copy-start.1 = (bf16[63,2048]{1,0:T(8,128)(2,1)S(1)}, bf16[63,2048]{1,0:T(8,128)(2,1)}, u32[]{:S(2)}) copy-start(bf16[63,2048]{1,0:T(8,128)(2,1)} %inv_hbm.1) | copy-start | bytes 774148
  0.7 7.6 %copy-start.2 = (bf16[10,2048]{1,0:T(8,128)(2,1)S(1)}, bf16[10,2048]{1,0:T(8,128)(2,1)}, u32[]{:S(2)}) copy-start(bf16[10,2048]{1,0:T(8,128)(2,1)} %pred_hbm.1) | copy-start | bytes 122884
  1.7 16.6 %collective-permute-start = (bf16[32,2048]{1,0:T(8,128)(2,1)S(1)}, bf16[32,2048]{1,0:T(8,128)(2,1)S(1)}, u32[]{:S(2)}, u32[]{:S(2)}) collective-permute-start(bf16[32,2048]{1,0:T(8,128)(2,1)S(1)} %get-tuple-element.12), channel_id=1, source_target_pairs={{0,1},{1,2},{2,3},{4,5},{5,6},{6,7},{8,9},{9,10},{10,11},{12,13},{... | collective-permute-start | bytes 393224 | tf_op jit(solution)/shard_map/ppermute | solution.py:279
  6.3 12.0 %collective-permute-start.1 = (bf16[32,2048]{1,0:T(8,128)(2,1)S(1)}, bf16[32,2048]{1,0:T(8,128)(2,1)S(1)}, u32[]{:S(2)}, u32[]{:S(2)}) collective-permute-start(bf16[32,2048]{1,0:T(8,128)(2,1)S(1)} %get-tuple-element.13), channel_id=1, source_target_pairs={{1,0},{2,1},{3,2},{5,4},{6,5},{7,6},{9,8},{10,9},{11,10},{13,12},{... | collective-permute-start | bytes 393224 | tf_op jit(solution)/shard_map/ppermute | solution.py:280
  18.4 30.5 %copy-start = (s32[1,128]{1,0:T(1,128)S(1)}, s32[1,128]{1,0:T(1,128)}, u32[]{:S(2)}) copy-start(s32[1,128]{1,0:T(1,128)} %constant.6.clone.place_ref) | copy-start | bytes 1540

commit v2 on v1

--- a/solution.py
+++ b/solution.py
@@ -10,6 +10,9 @@
 HALO = 32
 WIN = TILE + 2 * HALO
 STEP = 256
+PIECES = 16
+WAITS = (4,)
+AHEAD = 2
 OBS = 512
 GROUP = 32
 ROWS = 24
@@ -17,22 +20,22 @@
 f32, bf16 = jnp.float32, jnp.bfloat16
 
 
-def prepare_moments(pred, counts, w1_ref, w2_ref):
+def prepare_moments(pred, counts, w1_ref, rows_ref):
     count_pred, obs = pred.shape
     lines = counts.shape[0]
     slots = obs // lines
     pairs_n = count_pred * (count_pred + 1) // 2
+    offset = pairs_n % 8
     lane = lax.broadcasted_iota(jnp.int32, (1, slots), 1)
-    column = lax.broadcasted_iota(jnp.int32, (slots, 128), 1)
     for line in range(lines):
         at = slice(line * slots, (line + 1) * slots)
         p = jnp.where(lane < counts[line], pred[:, at].astype(f32), 0.0)
-        rows = [p[j : j + 1] * p[j:] for j in range(count_pred)] + [p]
-        used = pairs_n + count_pred
-        rows.append(jnp.zeros((128 - used, slots), f32))
-        moments = jnp.concatenate(rows, axis=0).T
-        w1_ref[at] = jnp.where(column < pairs_n, moments, 0.0).astype(bf16)
-        w2_ref[at] = jnp.where(column >= pairs_n, moments, 0.0).astype(bf16)
+        rows = [p[j : j + 1] * p[j:] for j in range(count_pred)]
+        rows.append(jnp.zeros((128 - pairs_n, slots), f32))
+        w1_ref[at] = jnp.concatenate(rows, axis=0).T.astype(bf16)
+        below = jnp.zeros((offset, slots), f32)
+        above = jnp.zeros((32 - offset - count_pred, slots), f32)
+        rows_ref[:, at] = jnp.concatenate([below, p, above], axis=0).astype(bf16)
 
 
 def prepare_band(t, chan, inv_ref, ids_ref, band_ref):
@@ -73,7 +76,13 @@
     lane = lax.broadcasted_iota(jnp.int32, (GROUP // 2, 128), 1)
     lane8 = lax.broadcasted_iota(jnp.int32, (8, 128), 1)
     total = jnp.dot(qc_ref[...], w1[...], preferred_element_type=f32)
-    total += jnp.dot(scaled_ref[...], w2[...], preferred_element_type=f32)
+    obs = scaled_ref.shape[1]
+    below = jnp.zeros((48, STEP), f32)
+    for at in (slice(0, obs // 2), slice(obs // 2, obs)):
+        turned = lax.dot_general(
+            w2[:, at], scaled_ref[:, at], (((1,), (1,)), ((), ())), preferred_element_type=f32
+        )
+        total += jnp.concatenate([below, turned, below], axis=0).T
     for g in range(STEP // GROUP):
         block = total[g * GROUP : (g + 1) * GROUP]
         low, high = block[: GROUP // 2], block[GROUP // 2 :]
@@ -97,7 +106,6 @@
     own, obs = dep_hbm.shape
     tiles = own // TILE
     steps = tiles // 2 - 1
-    chunks = own // STEP
 
     def copy(number, source, target):
         return pltpu.make_async_copy(source, target, sems.at[number])
@@ -108,12 +116,13 @@
         copy(2, inv_hbm, inv),
         copy(3, ids_hbm, ids),
     ]
-    rows = [pl.ds(s * STEP, STEP) for s in range(chunks)]
-    large = [copy(4 + s, dep_hbm.at[rows[s]], dep_all.at[rows[s]]) for s in range(chunks)]
+    cuts = [(n * own // PIECES) for n in range(PIECES + 1)]
+    rows = [pl.ds(a, b - a) for a, b in zip(cuts, cuts[1:])]
+    large = [copy(4 + n, dep_hbm.at[r], dep_all.at[r]) for n, r in enumerate(rows)]
     kept = WIN - HALO
     ends = [
-        copy(4 + chunks, dep_hbm.at[pl.ds(0, kept)], edge.at[0, pl.ds(HALO, kept)]),
-        copy(5 + chunks, dep_hbm.at[pl.ds(own - kept, kept)], edge.at[1, pl.ds(0, kept)]),
+        copy(4 + PIECES, dep_hbm.at[pl.ds(0, kept)], edge.at[0, pl.ds(HALO, kept)]),
+        copy(5 + PIECES, dep_hbm.at[pl.ds(own - kept, kept)], edge.at[1, pl.ds(0, kept)]),
     ]
     for c in small + large + ends:
         c.start()
@@ -121,28 +130,44 @@
         c.wait()
     chan = chan_ref[0]
     prepare_moments(pred, counts, w1, w2)
-    for t in range(tiles):
+
+    def prepare(t):
         if t == 0:
             prepare_band(t, chan, inv, ids, edge_band.at[0])
         elif t == tiles - 1:
             prepare_band(t, chan, inv, ids, edge_band.at[1])
         else:
             prepare_band(t, chan, inv, ids, band.at[t])
-    arrived = 0
-    for s in range(steps):
-        needed = min(chunks, ((2 * s + 3) * TILE + HALO - 1) // STEP + 1)
-        for c in large[arrived:needed]:
-            c.wait()
-        arrived = needed
+
+    def weigh_step(s):
         for half in range(2):
             t = 2 * s + 1 + half
             window = dep_all.at[pl.ds(t * TILE - HALO, WIN)]
             weigh(window, band.at[t], qc.at[s % 2], scaled.at[s % 2], pl.ds(half * TILE, TILE))
+
+    def reduce_step(s):
+        groups = groups_of(2 * s + 1, 2 * s + 2)
+        reduce(groups, qc.at[s % 2], scaled.at[s % 2], w1, w2, out_ref)
+
+    order = [(2 * s + 1, 2 * s + 2) for s in range(steps)] + [(0, tiles - 1)]
+    for pair in order[:AHEAD]:
+        prepare(pair[0])
+        prepare(pair[1])
+    arrived = 0
+    for s in range(steps):
         if s > 0:
-            p = s - 1
-            reduce(groups_of(2 * p + 1, 2 * p + 2), qc.at[p % 2], scaled.at[p % 2], w1, w2, out_ref)
-    p = steps - 1
-    reduce(groups_of(2 * p + 1, 2 * p + 2), qc.at[p % 2], scaled.at[p % 2], w1, w2, out_ref)
+            reduce_step(s - 1)
+        needed = next(n for n in range(PIECES + 1) if cuts[n] >= (2 * s + 3) * TILE + HALO)
+        if needed > arrived:
+            until = next((n for n in WAITS if n >= needed), PIECES)
+            for c in large[arrived:until]:
+                c.wait()
+            arrived = until
+        weigh_step(s)
+        for pair in order[s + AHEAD : s + AHEAD + 1]:
+            prepare(pair[0])
+            prepare(pair[1])
+    reduce_step(steps - 1)
     for c in large[arrived:] + ends:
         c.wait()
 
@@ -199,7 +224,7 @@
             edge_shape,
             shape((2, TILE, 256), bf16),
             shape((obs, 128), bf16),
-            shape((obs, 128), bf16),
+            shape((32, obs), bf16),
         ),
         in_specs=[smem, hbm, hbm, hbm, hbm, hbm],
         out_specs=(vmem,) * 5,
@@ -212,7 +237,7 @@
             pltpu.VMEM(pred.shape, bf16),
             pltpu.VMEM(inv_band.shape, bf16),
             pltpu.VMEM(ids.shape, jnp.int32),
-            pltpu.SemaphoreType.DMA((6 + own // STEP,)),
+            pltpu.SemaphoreType.DMA((6 + PIECES,)),
         ],
         compiler_params=pltpu.CompilerParams(vmem_limit_bytes=50 * 1024 * 1024),
         cost_estimate=pl.CostEstimate(flops=12_000_000_000, bytes_accessed=9_000_000, transcendentals=0),

time: 50 us -> 49.3 us (0.986)
  Pallas kernels: 13.1 us -> 12.6 us
    pallas_call x1, Pallas kernels: 10.1 us -> 9.51 us  [partial_sums(): pl.pallas_call(inner_kernel, out_shape=(parts_shape, edge_shape, shape((2...]
  transfers between devices with their start and end apart: 2 -> 2, of which waited for: 0 -> 0; matrix products, arithmetic and copies ran while one was open for 0% -> 0% of each run, Pallas kernels for 20% -> 19%
where the time goes in v2:
time: 49.3 us; the launch traced here: 49.1 us
  blocking collectives  29.2 us (59%)
  Pallas kernels  12.6 us (26%)
  starting transfers between devices  6.5 us (13%)
  between operations  0.76 us (2%)
    all_to_all x1, blocking collectives, on_device(): lax.all_to_all(parts, 'obs', split_axis=0, concat_axis=0, tiled=True)  29.2 us
    pallas_call x1, Pallas kernels, partial_sums(): pl.pallas_call(inner_kernel, out_shape=(parts_shape, edge_shape, shape((2...  9.51 us
    ppermute x1, starting transfers between devices, on_device(): top = lax.ppermute(tail, 'chan', up)  4.58 us
    ppermute x1, starting transfers between devices, on_device(): bottom = lax.ppermute(head, 'chan', down)  1.92 us
    pallas_call x1, Pallas kernels, partial_sums(): pl.pallas_call(edge_kernel, out_shape=(parts_shape, edge_shape), in_specs...  1.18 us
    pallas_call x1, Pallas kernels, borders(): pl.pallas_call(border_kernel, out_shape=(rows, rows), in_specs=[pl.BlockS...  1.03 us
  transfers between devices with their start and end apart: 2, of which 0 were waited for; matrix products, arithmetic and copies ran while one was open for 0% of the time, Pallas kernels for 19%

profile of v2, /device:TPU:1, one launch (start us, length us, event | category | flops | bytes accessed | tf_op | source)
XLA Modules:
  0.0 49.1 jit_solution(17827160692735208557)
XLA Ops:
  0.6 0.0 copy-start.4
  0.6 0.0 copy-start.3
  0.7 0.0 copy-start.1
  0.7 0.0 copy-start.2
  0.7 1.0 %borders.1 = (bf16[32,2048]{1,0:T(8,128)(2,1)S(1)}, bf16[32,2048]{1,0:T(8,128)(2,1)S(1)}) custom-call(bf16[2048,2048]{1,0:T(8,128)(2,1)} %dep_hbm.3), custom_call_target="tpu_custom_call" | custom-call | flops 20000000000 | bytes 500000 | tf_op jit(solution)/shard_map/borders/pallas_call | solution.py:199
  1.7 4.6 %collective-permute-start = (bf16[32,2048]{1,0:T(8,128)(2,1)S(1)}, bf16[32,2048]{1,0:T(8,128)(2,1)S(1)}, u32[]{:S(2)}, u32[]{:S(2)}) collective-permute-start(bf16[32,2048]{1,0:T(8,128)(2,1)S(1)} %get-tuple-element.12), channel_id=1, source_target_pairs={{0,1},{1,2},{2,3},{4,5},{5,6},{6,7},{8,9},{9,10},{10,11},{12,13},{... | collective-permute-start | bytes 393224 | tf_op jit(solution)/shard_map/ppermute | solution.py:304
  6.3 1.9 %collective-permute-start.1 = (bf16[32,2048]{1,0:T(8,128)(2,1)S(1)}, bf16[32,2048]{1,0:T(8,128)(2,1)S(1)}, u32[]{:S(2)}, u32[]{:S(2)}) collective-permute-start(bf16[32,2048]{1,0:T(8,128)(2,1)S(1)} %get-tuple-element.13), channel_id=1, source_target_pairs={{1,0},{2,1},{3,2},{5,4},{6,5},{7,6},{9,8},{10,9},{11,10},{13,12},{... | collective-permute-start | bytes 393224 | tf_op jit(solution)/shard_map/ppermute | solution.py:305
  8.2 0.0 copy-done.4
  8.2 0.0 copy-done.3
  8.3 0.0 copy-done.1
  8.3 0.0 copy-done.2
  8.3 9.5 %inner.1 = (bf16[64,24,128]{2,1,0:T(8,128)(2,1)S(1)}, bf16[2,192,2048]{2,1,0:T(8,128)(2,1)S(1)}, bf16[2,128,256]{2,1,0:T(8,128)(2,1)S(1)}, bf16[2048,128]{1,0:T(8,128)(2,1)S(1)}, bf16[32,2048]{1,0:T(8,128)(2,1)S(1)}) custom-call(s32[1]{0:T(128)} %bitcast.chan_ref, s32[16]{0:T(128)S(1)} %copy-done.4, bf16[10,2048]{1,0:T(8,128)(2,1)S(1)} %copy-done.2, ...), custom_call_target="tpu_custom_call" | custom-call | flops 12000000000 | bytes 9000000 | tf_op jit(solution)/shard_map/inner/pallas_call | solution.py:220
  17.8 0.0 collective-permute-done.top_ref
  17.8 0.0 collective-permute-done.1.bottom_ref
  17.8 0.0 copy-start
  17.8 1.2 %edge.1 = (bf16[64,24,128]{2,1,0:T(8,128)(2,1)S(1)}, bf16[2,192,2048]{2,1,0:T(8,128)(2,1)S(1)}) custom-call(bf16[32,2048]{1,0:T(8,128)(2,1)S(1)} %collective-permute-done.top_ref, bf16[32,2048]{1,0:T(8,128)(2,1)S(1)} %collective-permute-done.1.bottom_ref, ...), custom_call_target="tpu_custom_call", output_to_operand_aliasing={{0}: (5, {}), {1}: (6, {})} | custom-call | tf_op jit(solution)/shard_map/edge/pallas_call | solution.py:246
  19.0 29.2 %all_to_all.5.parts_ref = bf16[64,24,128]{2,1,0:T(8,128)(2,1)S(1)} all-to-all(bf16[64,24,128]{2,1,0:T(8,128)(2,1)S(1)} %get-tuple-element.19), channel_id=1, replica_groups=mesh['obs'=64,'chan'=4] {'obs'}, dimensions={0} | all-to-all | bytes 786432 | tf_op jit(solution)/shard_map/all_to_all | solution.py:309
  48.2 0.0 copy-done
  48.2 0.9 %finish.1 = (f32[32,100]{1,0:T(8,128)}, f32[10,32]{1,0:T(8,128)}) custom-call(s32[1,128]{1,0:T(1,128)S(1)} %copy-done, bf16[64,24,128]{2,1,0:T(8,128)(2,1)S(1)} %all_to_all.5.parts_ref), custom_call_target="tpu_custom_call" | custom-call | tf_op jit(solution)/shard_map/finish/pallas_call | solution.py:284
Async XLA Ops:
  0.6 7.6 %copy-start.4 = (s32[16]{0:T(128)S(1)}, s32[16]{0:T(128)}, u32[]{:S(2)}) copy-start(s32[16]{0:T(128)} %counts_hbm.1) | copy-start | bytes 196
  0.6 7.6 %copy-start.3 = (s32[8192]{0:T(1024)S(1)}, s32[8192]{0:T(1024)}, u32[]{:S(2)}) copy-start(s32[8192]{0:T(1024)} %param.9) | copy-start | bytes 98308
  0.7 7.6 %copy-start.1 = (bf16[63,2048]{1,0:T(8,128)(2,1)S(1)}, bf16[63,2048]{1,0:T(8,128)(2,1)}, u32[]{:S(2)}) copy-start(bf16[63,2048]{1,0:T(8,128)(2,1)} %inv_hbm.1) | copy-start | bytes 774148
  0.7 7.6 %copy-start.2 = (bf16[10,2048]{1,0:T(8,128)(2,1)S(1)}, bf16[10,2048]{1,0:T(8,128)(2,1)}, u32[]{:S(2)}) copy-start(bf16[10,2048]{1,0:T(8,128)(2,1)} %pred_hbm.1) | copy-start | bytes 122884
  1.7 16.1 %collective-permute-start = (bf16[32,2048]{1,0:T(8,128)(2,1)S(1)}, bf16[32,2048]{1,0:T(8,128)(2,1)S(1)}, u32[]{:S(2)}, u32[]{:S(2)}) collective-permute-start(bf16[32,2048]{1,0:T(8,128)(2,1)S(1)} %get-tuple-element.12), channel_id=1, source_target_pairs={{0,1},{1,2},{2,3},{4,5},{5,6},{6,7},{8,9},{9,10},{10,11},{12,13},{... | collective-permute-start | bytes 393224 | tf_op jit(solution)/shard_map/ppermute | solution.py:304
  6.3 11.5 %collective-permute-start.1 = (bf16[32,2048]{1,0:T(8,128)(2,1)S(1)}, bf16[32,2048]{1,0:T(8,128)(2,1)S(1)}, u32[]{:S(2)}, u32[]{:S(2)}) collective-permute-start(bf16[32,2048]{1,0:T(8,128)(2,1)S(1)} %get-tuple-element.13), channel_id=1, source_target_pairs={{1,0},{2,1},{3,2},{5,4},{6,5},{7,6},{9,8},{10,9},{11,10},{13,12},{... | collective-permute-start | bytes 393224 | tf_op jit(solution)/shard_map/ppermute | solution.py:305
  17.8 30.4 %copy-start = (s32[1,128]{1,0:T(1,128)S(1)}, s32[1,128]{1,0:T(1,128)}, u32[]{:S(2)}) copy-start(s32[1,128]{1,0:T(1,128)} %constant.6.clone.place_ref) | copy-start | bytes 1540

commit v3 on v2

--- a/solution.py
+++ b/solution.py
@@ -10,8 +10,8 @@
 HALO = 32
 WIN = TILE + 2 * HALO
 STEP = 256
-PIECES = 16
-WAITS = (4,)
+PIECES = 8
+WAITS = (2, 4)
 AHEAD = 2
 OBS = 512
 GROUP = 32
@@ -99,9 +99,9 @@
 
 
 def inner_kernel(
-    chan_ref, counts_hbm, pred_hbm, inv_hbm, ids_hbm, dep_hbm,
+    counts_hbm, pred, inv, ids, dep_hbm,
     out_ref, edge, edge_band, w1, w2,
-    dep_all, band, qc, scaled, counts, pred, inv, ids, sems,
+    dep_all, band, qc, scaled, counts, sems,
 ):
     own, obs = dep_hbm.shape
     tiles = own // TILE
@@ -110,25 +110,20 @@
     def copy(number, source, target):
         return pltpu.make_async_copy(source, target, sems.at[number])
 
-    small = [
-        copy(0, counts_hbm, counts),
-        copy(1, pred_hbm, pred),
-        copy(2, inv_hbm, inv),
-        copy(3, ids_hbm, ids),
-    ]
+    small = [copy(0, counts_hbm, counts)]
     cuts = [(n * own // PIECES) for n in range(PIECES + 1)]
     rows = [pl.ds(a, b - a) for a, b in zip(cuts, cuts[1:])]
-    large = [copy(4 + n, dep_hbm.at[r], dep_all.at[r]) for n, r in enumerate(rows)]
+    large = [copy(1 + n, dep_hbm.at[r], dep_all.at[r]) for n, r in enumerate(rows)]
     kept = WIN - HALO
     ends = [
-        copy(4 + PIECES, dep_hbm.at[pl.ds(0, kept)], edge.at[0, pl.ds(HALO, kept)]),
-        copy(5 + PIECES, dep_hbm.at[pl.ds(own - kept, kept)], edge.at[1, pl.ds(0, kept)]),
+        copy(1 + PIECES, dep_hbm.at[pl.ds(0, kept)], edge.at[0, pl.ds(HALO, kept)]),
+        copy(2 + PIECES, dep_hbm.at[pl.ds(own - kept, kept)], edge.at[1, pl.ds(0, kept)]),
     ]
     for c in small + large + ends:
         c.start()
     for c in small:
         c.wait()
-    chan = chan_ref[0]
+    chan = lax.axis_index("chan").astype(jnp.int32)
     prepare_moments(pred, counts, w1, w2)
 
     def prepare(t):
@@ -208,11 +203,10 @@
     )(departures)
 
 
-def partial_sums(chan, counts, top, bottom, pred, inv_band, ids, departures):
+def partial_sums(counts, top, bottom, pred, inv_band, ids, departures):
     own, obs = departures.shape
     tiles = own // TILE
     vmem = pl.BlockSpec(memory_space=pltpu.VMEM)
-    smem = pl.BlockSpec(memory_space=pltpu.SMEM)
     hbm = pl.BlockSpec(memory_space=pltpu.HBM)
     shape = jax.ShapeDtypeStruct
     parts_shape = shape((own // GROUP, ROWS, 128), bf16)
@@ -226,7 +220,7 @@
             shape((obs, 128), bf16),
             shape((32, obs), bf16),
         ),
-        in_specs=[smem, hbm, hbm, hbm, hbm, hbm],
+        in_specs=[hbm, vmem, vmem, vmem, hbm],
         out_specs=(vmem,) * 5,
         scratch_shapes=[
             pltpu.VMEM((own, obs), bf16),
@@ -234,15 +228,12 @@
             pltpu.VMEM((2, STEP, obs), bf16),
             pltpu.VMEM((2, STEP, obs), bf16),
             pltpu.SMEM(counts.shape, jnp.int32),
-            pltpu.VMEM(pred.shape, bf16),
-            pltpu.VMEM(inv_band.shape, bf16),
-            pltpu.VMEM(ids.shape, jnp.int32),
-            pltpu.SemaphoreType.DMA((6 + PIECES,)),
+            pltpu.SemaphoreType.DMA((3 + PIECES,)),
         ],
         compiler_params=pltpu.CompilerParams(vmem_limit_bytes=50 * 1024 * 1024),
         cost_estimate=pl.CostEstimate(flops=12_000_000_000, bytes_accessed=9_000_000, transcendentals=0),
         name="inner",
-    )(chan, counts, pred, inv_band, ids, departures)
+    )(counts, pred, inv_band, ids, departures)
     parts, _ = pl.pallas_call(
         edge_kernel,
         out_shape=(parts_shape, edge_shape),
@@ -303,9 +294,8 @@
     head, tail = borders(departures)
     top = lax.ppermute(tail, "chan", up)
     bottom = lax.ppermute(head, "chan", down)
-    chan = lax.axis_index("chan").astype(jnp.int32).reshape(1)
     ids = band_id.reshape(-1, TILE)
-    parts = partial_sums(chan, line_counts, top, bottom, predictors, inv_band, ids, departures)
+    parts = partial_sums(line_counts, top, bottom, predictors, inv_band, ids, departures)
     arrived = lax.all_to_all(parts, "obs", split_axis=0, concat_axis=0, tiled=True)
     return finish(arrived, predictors.shape[0], 1.0 / float(obs * lax.axis_size("obs")))
 

time: 49.3 us -> 48.9 us (level)
  no operation moved by 1% of the time
where the time goes in v3:
time: 48.9 us; the launch traced here: 48.7 us
  blocking collectives  29.2 us (60%)
  Pallas kernels  12.2 us (25%)
  starting transfers between devices  6.5 us (13%)
  between operations  0.76 us (2%)
    all_to_all x1, blocking collectives, on_device(): lax.all_to_all(parts, 'obs', split_axis=0, concat_axis=0, tiled=True)  29.2 us
    pallas_call x1, Pallas kernels, partial_sums(): pl.pallas_call(inner_kernel, out_shape=(parts_shape, edge_shape, shape((2...  9.09 us
    ppermute x1, starting transfers between devices, on_device(): top = lax.ppermute(tail, 'chan', up)  4.58 us
    ppermute x1, starting transfers between devices, on_device(): bottom = lax.ppermute(head, 'chan', down)  1.92 us
    pallas_call x1, Pallas kernels, partial_sums(): pl.pallas_call(edge_kernel, out_shape=(parts_shape, edge_shape), in_specs...  1.18 us
    pallas_call x1, Pallas kernels, borders(): pl.pallas_call(border_kernel, out_shape=(rows, rows), in_specs=[pl.BlockS...  1.03 us
  transfers between devices with their start and end apart: 2, of which 0 were waited for; matrix products, arithmetic and copies ran while one was open for 0% of the time, Pallas kernels for 19%

profile of v3, /device:TPU:1, one launch (start us, length us, event | category | flops | bytes accessed | tf_op | source)
XLA Modules:
  0.0 48.7 jit_solution(15067394285828429016)
XLA Ops:
  0.6 0.0 copy-start.4
  0.6 0.0 copy-start.3
  0.7 0.0 copy-start.1
  0.7 0.0 copy-start.2
  0.7 1.0 %borders.1 = (bf16[32,2048]{1,0:T(8,128)(2,1)S(1)}, bf16[32,2048]{1,0:T(8,128)(2,1)S(1)}) custom-call(bf16[2048,2048]{1,0:T(8,128)(2,1)} %dep_hbm.3), custom_call_target="tpu_custom_call" | custom-call | flops 20000000000 | bytes 500000 | tf_op jit(solution)/shard_map/borders/pallas_call | solution.py:194
  1.7 4.6 %collective-permute-start = (bf16[32,2048]{1,0:T(8,128)(2,1)S(1)}, bf16[32,2048]{1,0:T(8,128)(2,1)S(1)}, u32[]{:S(2)}, u32[]{:S(2)}) collective-permute-start(bf16[32,2048]{1,0:T(8,128)(2,1)S(1)} %get-tuple-element.12), channel_id=1, source_target_pairs={{0,1},{1,2},{2,3},{4,5},{5,6},{6,7},{8,9},{9,10},{10,11},{12,13},{... | collective-permute-start | bytes 393224 | tf_op jit(solution)/shard_map/ppermute | solution.py:295
  6.3 1.9 %collective-permute-start.1 = (bf16[32,2048]{1,0:T(8,128)(2,1)S(1)}, bf16[32,2048]{1,0:T(8,128)(2,1)S(1)}, u32[]{:S(2)}, u32[]{:S(2)}) collective-permute-start(bf16[32,2048]{1,0:T(8,128)(2,1)S(1)} %get-tuple-element.13), channel_id=1, source_target_pairs={{1,0},{2,1},{3,2},{5,4},{6,5},{7,6},{9,8},{10,9},{11,10},{13,12},{... | collective-permute-start | bytes 393224 | tf_op jit(solution)/shard_map/ppermute | solution.py:296
  8.2 0.0 copy-done.4
  8.2 0.0 copy-done.3
  8.3 0.0 copy-done.1
  8.3 0.0 copy-done.2
  8.3 9.1 %inner.1 = (bf16[64,24,128]{2,1,0:T(8,128)(2,1)S(1)}, bf16[2,192,2048]{2,1,0:T(8,128)(2,1)S(1)}, bf16[2,128,256]{2,1,0:T(8,128)(2,1)S(1)}, bf16[2048,128]{1,0:T(8,128)(2,1)S(1)}, bf16[32,2048]{1,0:T(8,128)(2,1)S(1)}) custom-call(s32[16]{0:T(128)S(1)} %copy-done.4, bf16[10,2048]{1,0:T(8,128)(2,1)S(1)} %copy-done.2, bf16[63,2048]{1,0:T(8,128)(2,1)S(1)} %copy-done.1, ...), custom_call_target="tpu_custom_call" | custom-call | flops 12000000000 | bytes 9000000 | tf_op jit(solution)/shard_map/inner/pallas_call | solution.py:214
  17.4 0.0 collective-permute-done.top_ref
  17.4 0.0 collective-permute-done.1.bottom_ref
  17.4 0.0 copy-start
  17.4 1.2 %edge.1 = (bf16[64,24,128]{2,1,0:T(8,128)(2,1)S(1)}, bf16[2,192,2048]{2,1,0:T(8,128)(2,1)S(1)}) custom-call(bf16[32,2048]{1,0:T(8,128)(2,1)S(1)} %collective-permute-done.top_ref, bf16[32,2048]{1,0:T(8,128)(2,1)S(1)} %collective-permute-done.1.bottom_ref, ...), custom_call_target="tpu_custom_call", output_to_operand_aliasing={{0}: (5, {}), {1}: (6, {})} | custom-call | tf_op jit(solution)/shard_map/edge/pallas_call | solution.py:237
  18.6 29.2 %all_to_all.5.parts_ref = bf16[64,24,128]{2,1,0:T(8,128)(2,1)S(1)} all-to-all(bf16[64,24,128]{2,1,0:T(8,128)(2,1)S(1)} %get-tuple-element.19), channel_id=1, replica_groups=mesh['obs'=64,'chan'=4] {'obs'}, dimensions={0} | all-to-all | bytes 786432 | tf_op jit(solution)/shard_map/all_to_all | solution.py:299
  47.8 0.0 copy-done
  47.8 0.9 %finish.1 = (f32[32,100]{1,0:T(8,128)}, f32[10,32]{1,0:T(8,128)}) custom-call(s32[1,128]{1,0:T(1,128)S(1)} %copy-done, bf16[64,24,128]{2,1,0:T(8,128)(2,1)S(1)} %all_to_all.5.parts_ref), custom_call_target="tpu_custom_call" | custom-call | tf_op jit(solution)/shard_map/finish/pallas_call | solution.py:275
Async XLA Ops:
  0.6 7.6 %copy-start.4 = (s32[16]{0:T(128)S(1)}, s32[16]{0:T(128)}, u32[]{:S(2)}) copy-start(s32[16]{0:T(128)} %counts_hbm.1) | copy-start | bytes 196
  0.6 7.6 %copy-start.3 = (s32[8192]{0:T(1024)S(1)}, s32[8192]{0:T(1024)}, u32[]{:S(2)}) copy-start(s32[8192]{0:T(1024)} %param.9) | copy-start | bytes 98308
  0.7 7.6 %copy-start.1 = (bf16[63,2048]{1,0:T(8,128)(2,1)S(1)}, bf16[63,2048]{1,0:T(8,128)(2,1)}, u32[]{:S(2)}) copy-start(bf16[63,2048]{1,0:T(8,128)(2,1)} %inv.1) | copy-start | bytes 774148
  0.7 7.6 %copy-start.2 = (bf16[10,2048]{1,0:T(8,128)(2,1)S(1)}, bf16[10,2048]{1,0:T(8,128)(2,1)}, u32[]{:S(2)}) copy-start(bf16[10,2048]{1,0:T(8,128)(2,1)} %pred_.1) | copy-start | bytes 122884
  1.7 15.7 %collective-permute-start = (bf16[32,2048]{1,0:T(8,128)(2,1)S(1)}, bf16[32,2048]{1,0:T(8,128)(2,1)S(1)}, u32[]{:S(2)}, u32[]{:S(2)}) collective-permute-start(bf16[32,2048]{1,0:T(8,128)(2,1)S(1)} %get-tuple-element.12), channel_id=1, source_target_pairs={{0,1},{1,2},{2,3},{4,5},{5,6},{6,7},{8,9},{9,10},{10,11},{12,13},{... | collective-permute-start | bytes 393224 | tf_op jit(solution)/shard_map/ppermute | solution.py:295
  6.3 11.1 %collective-permute-start.1 = (bf16[32,2048]{1,0:T(8,128)(2,1)S(1)}, bf16[32,2048]{1,0:T(8,128)(2,1)S(1)}, u32[]{:S(2)}, u32[]{:S(2)}) collective-permute-start(bf16[32,2048]{1,0:T(8,128)(2,1)S(1)} %get-tuple-element.13), channel_id=1, source_target_pairs={{1,0},{2,1},{3,2},{5,4},{6,5},{7,6},{9,8},{10,9},{11,10},{13,12},{... | collective-permute-start | bytes 393224 | tf_op jit(solution)/shard_map/ppermute | solution.py:296
  17.4 30.4 %copy-start = (s32[1,128]{1,0:T(1,128)S(1)}, s32[1,128]{1,0:T(1,128)}, u32[]{:S(2)}) copy-start(s32[1,128]{1,0:T(1,128)} %constant.2.clone.place_ref) | copy-start | bytes 1540
